TPU v7x, 64 devices: a 2x2x8 block of a 4x4x8 slice. The times are simulated.
64 devices in a mesh: dp: 4 (over x, y), cp: 16 (over z, core).
Axes of the slice: x: 2, y: 2, z: 8, core: 2. Of those that a mesh axis runs over, the one named last changes fastest.
The devices are a block of a 4x4x8 slice.
Arguments:
- query: bfloat16 [64, 1024, 16, 128], P('dp', 'cp'), parts along dimension 0
- keys: bfloat16 [64, 1024, 1, 128], P('dp', 'cp'), parts along dimension 0
- values: bfloat16 [64, 1024, 1, 128], P('dp', 'cp'), parts along dimension 0
- grad_out: bfloat16 [64, 1024, 16, 128], P('dp', 'cp'), parts along dimension 0
- doc_id: int32 [64, 1024], P('dp', 'cp'), parts along dimension 0
Outputs:
- output 1: bfloat16 [64, 1024, 16, 128], P('dp', 'cp'), parts along dimension 0
- output 2: bfloat16 [64, 1024, 16, 128], P('dp', 'cp'), parts along dimension 0
- output 3: bfloat16 [64, 1024, 1, 128], P('dp', 'cp'), parts along dimension 0
- output 4: bfloat16 [64, 1024, 1, 128], P('dp', 'cp'), parts along dimension 0
There are 4 independent parts. A program takes and returns all parts, laid end to end along the dimension named above; each array names one.
All inputs are finite; a program needn't handle non-finite values.
Results may differ from a plain program's by a relative error of at most 0.0108808.
Values are sent between devices in bfloat16 or wider.
A program may use at most 768 MiB of HBM per device.

v0:
```python
import jax
import jax.numpy as jnp
from jax import lax
from jax.sharding import PartitionSpec as P, NamedSharding

NEG_BIG = -1e30


def solution(mesh):
    n_grp = mesh.shape['cp']
    to_next = [(src_dev, (src_dev + 1) % n_grp) for src_dev in range(n_grp)]
    seq_spec = P('dp', 'cp', None, None)
    id_spec = P('dp', 'cp')

    def per_device(query, keys, values, grad_out, doc_id):
        n_batch, piece_len, n_heads, head_dim = query.shape
        score_scale = head_dim ** -0.5
        dev_rank = lax.axis_index('cp')
        offsets = jnp.arange(piece_len)
        q_pos = dev_rank * piece_len + offsets
        key_loc = keys[:, :, 0, :]
        val_loc = values[:, :, 0, :]

        def masked_scores(step, key_cur, doc_cur):
            src_rank = (dev_rank - step) % n_grp
            k_pos = src_rank * piece_len + offsets
            causal = k_pos[None, :] <= q_pos[:, None]
            same_doc = doc_id[:, :, None] == doc_cur[:, None, :]
            visible = (causal[None] & same_doc)[:, :, None, :]
            raw_scores = jnp.einsum('crie,cle->cril', query, key_cur, preferred_element_type=jnp.float32)
            return jnp.where(visible, raw_scores * score_scale, NEG_BIG), visible

        def stats_update(step, key_cur, doc_cur, row_max, row_sum):
            scores, visible = masked_scores(step, key_cur, doc_cur)
            new_max = jnp.maximum(row_max, jnp.max(scores, axis=-1))
            exp_scores = jnp.where(visible, jnp.exp(scores - new_max[..., None]), 0.0)
            new_sum = row_sum * jnp.exp(row_max - new_max) + jnp.sum(exp_scores, axis=-1)
            return new_max, new_sum

        def stats_body(step, carry):
            key_cur, doc_cur, row_max, row_sum = carry
            key_cur = lax.ppermute(key_cur, 'cp', to_next)
            doc_cur = lax.ppermute(doc_cur, 'cp', to_next)
            row_max, row_sum = stats_update(step, key_cur, doc_cur, row_max, row_sum)
            return key_cur, doc_cur, row_max, row_sum

        stat_shape = (n_batch, piece_len, n_heads)
        row_max, row_sum = stats_update(0, key_loc, doc_id, jnp.full(stat_shape, NEG_BIG, jnp.float32), jnp.zeros(stat_shape, jnp.float32))
        stats_out = lax.fori_loop(1, n_grp, stats_body, (key_loc, doc_id, row_max, row_sum))
        log_norm = stats_out[2] + jnp.log(stats_out[3])

        def prob_at(step, key_cur, doc_cur):
            scores = masked_scores(step, key_cur, doc_cur)[0]
            return jnp.exp(scores - log_norm[..., None])

        def out_update(step, key_cur, val_cur, doc_cur, out_acc):
            prob_bf16 = prob_at(step, key_cur, doc_cur).astype(jnp.bfloat16)
            return out_acc + jnp.einsum('cril,cle->crie', prob_bf16, val_cur, preferred_element_type=jnp.float32)

        def out_body(step, carry):
            key_cur, val_cur, doc_cur, out_acc = carry
            key_cur = lax.ppermute(key_cur, 'cp', to_next)
            val_cur = lax.ppermute(val_cur, 'cp', to_next)
            doc_cur = lax.ppermute(doc_cur, 'cp', to_next)
            return key_cur, val_cur, doc_cur, out_update(step, key_cur, val_cur, doc_cur, out_acc)

        out_acc = out_update(0, key_loc, val_loc, doc_id, jnp.zeros(query.shape, jnp.float32))
        out_acc = lax.fori_loop(1, n_grp, out_body, (key_loc, val_loc, doc_id, out_acc))[3]
        attn_out = out_acc.astype(jnp.bfloat16)
        row_delta = jnp.einsum('bqhd,bqhd->bqh', grad_out, attn_out, preferred_element_type=jnp.float32)

        def grad_update(step, key_cur, val_cur, doc_cur, dq_acc, dk_acc, dv_acc):
            prob_f32 = prob_at(step, key_cur, doc_cur)
            prob_bf16 = prob_f32.astype(jnp.bfloat16)
            grad_prob = jnp.einsum('crie,cle->cril', grad_out, val_cur, preferred_element_type=jnp.float32)
            grad_score = (prob_f32 * (grad_prob - row_delta[..., None])).astype(jnp.bfloat16)
            dq_acc = dq_acc + jnp.einsum('cril,cle->crie', grad_score, key_cur, preferred_element_type=jnp.float32)
            dk_acc = dk_acc + jnp.einsum('cril,crie->cle', grad_score, query, preferred_element_type=jnp.float32)
            dv_acc = dv_acc + jnp.einsum('cril,crie->cle', prob_bf16, grad_out, preferred_element_type=jnp.float32)
            return dq_acc, dk_acc, dv_acc

        def grad_body(step, carry):
            key_cur, val_cur, doc_cur, dq_acc, dk_acc, dv_acc = carry
            key_cur = lax.ppermute(key_cur, 'cp', to_next)
            val_cur = lax.ppermute(val_cur, 'cp', to_next)
            doc_cur = lax.ppermute(doc_cur, 'cp', to_next)
            dk_acc = lax.ppermute(dk_acc, 'cp', to_next)
            dv_acc = lax.ppermute(dv_acc, 'cp', to_next)
            dq_acc, dk_acc, dv_acc = grad_update(step, key_cur, val_cur, doc_cur, dq_acc, dk_acc, dv_acc)
            return key_cur, val_cur, doc_cur, dq_acc, dk_acc, dv_acc

        kv_zero = jnp.zeros(key_loc.shape, jnp.float32)
        grads = grad_update(0, key_loc, val_loc, doc_id, jnp.zeros(query.shape, jnp.float32), kv_zero, kv_zero)
        grads = lax.fori_loop(1, n_grp, grad_body, (key_loc, val_loc, doc_id) + grads)
        dk_home = lax.ppermute(grads[4], 'cp', to_next)
        dv_home = lax.ppermute(grads[5], 'cp', to_next)
        grad_query = (grads[3] * score_scale).astype(jnp.bfloat16)
        grad_keys = (dk_home * score_scale).astype(jnp.bfloat16)[:, :, None, :]
        grad_values = dv_home.astype(jnp.bfloat16)[:, :, None, :]
        return attn_out, grad_query, grad_keys, grad_values

    return jax.shard_map(per_device, mesh=mesh, in_specs=(seq_spec, seq_spec, seq_spec, seq_spec, id_spec), out_specs=(seq_spec, seq_spec, seq_spec, seq_spec), check_vma=False)
```

profile of v0, /device:TPU:21, one launch (start us, length us, event | category | flops | bytes accessed | tf_op | source)
XLA Modules:
  0.0 1193.4 jit_solution(4666574437693483654)
XLA Ops:
  19.2 273.7 %while.70 = (s32[]{:T(128)}, bf16[16,64,128]{2,1,0:T(8,128)(2,1)S(1)}, s32[16,64]{1,0:T(8,128)S(1)}, f32[16,64,16]{2,1,0:T(8,128)S(1)}, f32[16,64,16]{2,1,0:T(8,...) while((s32[]{:T(128)}, ...), condition=%wide.region_5.6_spmd.clone, body=%wide.region_2.5_spmd.clone.sunk | while | flops 276992128 | bytes 15508834 | solution.py:49
  302.3 290.9 %while.71 = (s32[]{:T(128)}, bf16[16,64,128]{2,1,0:T(8,128)(2,1)S(1)}, bf16[16,64,128]{2,1,0:T(8,128)(2,1)S(1)}, s32[16,64]{1,0:T(8,128)S(1)}, f32[16,64,16,128]...) while((s32[]{:T(128)}, ...), condition=%wide.region_7.8_spmd.clone, body=%wide.region_6.7_spmd.clone.sunk | while | flops 543297664 | bytes 24880528 | solution.py:68
  309.9 9.6 fusion.100
  329.4 9.6 fusion.100
  349.0 9.6 fusion.100
  368.5 9.6 fusion.100
  388.1 9.6 fusion.100
  407.6 9.6 fusion.100
  427.2 9.6 fusion.100
  446.7 9.6 fusion.100
  466.3 9.6 fusion.100
  485.9 9.6 fusion.100
  505.4 9.6 fusion.100
  525.0 9.6 fusion.100
  544.5 9.6 fusion.100
  564.1 9.6 fusion.100
  583.6 9.6 fusion.100
  632.2 548.2 %while.72 = (s32[]{:T(128)}, bf16[16,64,128]{2,1,0:T(8,128)(2,1)S(1)}, bf16[16,64,128]{2,1,0:T(8,128)(2,1)S(1)}, s32[16,64]{1,0:T(8,128)S(1)}, f32[16,64,16,128]...) while((s32[]{:T(128)}, ...), condition=%wide.region_9.10_spmd.clone, body=%wide.region_8.9_spmd.clone.sunk | while | flops 1355157632 | bytes 155362960 | solution.py:94
  716.0 9.4 fusion.109
  752.5 9.4 fusion.109
  789.0 9.4 fusion.109
  825.5 9.4 fusion.109
  862.0 9.4 fusion.109
  898.5 9.4 fusion.109
  (954 shorter events, 988.5 us)
Async XLA Ops:
  639.8 26.9 %collective-permute-start.9 = (f32[16,64,128]{2,1,0:T(8,128)S(1)}, f32[16,64,128]{2,1,0:T(8,128)}, u32[]{:S(2)}, u32[]{:S(2)}) collective-permute-start(f32[16,64,128]{2,1,0:T(8,128)S(1)} %get-tuple-element.1363), channel_id=1, source_target_pairs={{0,1},{1,2},{2,3},{3,4},{4,5},{5,6},{6,7},{7,8},{8,9},{9,10},{10,1... | collective-permute-start | bytes 1572872 | tf_op jit(solution)/shard_map/while/body/eval_jaxpr/ppermute | solution.py:88
  675.0 24.1 %collective-permute-start.8 = (f32[16,64,128]{2,1,0:T(8,128)}, f32[16,64,128]{2,1,0:T(8,128)}, u32[]{:S(2)}, u32[]{:S(2)}) collective-permute-start(f32[16,64,128]{2,1,0:T(8,128)} %get-tuple-element.1362), channel_id=1, source_target_pairs={{0,1},{1,2},{2,3},{3,4},{4,5},{5,6},{6,7},{7,8},{8,9},{9,10},{10,1... | collective-permute-start | bytes 1572872 | tf_op jit(solution)/shard_map/while/body/eval_jaxpr/ppermute | solution.py:87
  676.3 27.2 %collective-permute-start.9 = (f32[16,64,128]{2,1,0:T(8,128)S(1)}, f32[16,64,128]{2,1,0:T(8,128)}, u32[]{:S(2)}, u32[]{:S(2)}) collective-permute-start(f32[16,64,128]{2,1,0:T(8,128)S(1)} %get-tuple-element.1363), channel_id=1, source_target_pairs={{0,1},{1,2},{2,3},{3,4},{4,5},{5,6},{6,7},{7,8},{8,9},{9,10},{10,1... | collective-permute-start | bytes 1572872 | tf_op jit(solution)/shard_map/while/body/eval_jaxpr/ppermute | solution.py:88
  712.8 27.2 %collective-permute-start.9 = (f32[16,64,128]{2,1,0:T(8,128)S(1)}, f32[16,64,128]{2,1,0:T(8,128)}, u32[]{:S(2)}, u32[]{:S(2)}) collective-permute-start(f32[16,64,128]{2,1,0:T(8,128)S(1)} %get-tuple-element.1363), channel_id=1, source_target_pairs={{0,1},{1,2},{2,3},{3,4},{4,5},{5,6},{6,7},{7,8},{8,9},{9,10},{10,1... | collective-permute-start | bytes 1572872 | tf_op jit(solution)/shard_map/while/body/eval_jaxpr/ppermute | solution.py:88
  749.3 27.2 %collective-permute-start.9 = (f32[16,64,128]{2,1,0:T(8,128)S(1)}, f32[16,64,128]{2,1,0:T(8,128)}, u32[]{:S(2)}, u32[]{:S(2)}) collective-permute-start(f32[16,64,128]{2,1,0:T(8,128)S(1)} %get-tuple-element.1363), channel_id=1, source_target_pairs={{0,1},{1,2},{2,3},{3,4},{4,5},{5,6},{6,7},{7,8},{8,9},{9,10},{10,1... | collective-permute-start | bytes 1572872 | tf_op jit(solution)/shard_map/while/body/eval_jaxpr/ppermute | solution.py:88
  785.8 27.2 %collective-permute-start.9 = (f32[16,64,128]{2,1,0:T(8,128)S(1)}, f32[16,64,128]{2,1,0:T(8,128)}, u32[]{:S(2)}, u32[]{:S(2)}) collective-permute-start(f32[16,64,128]{2,1,0:T(8,128)S(1)} %get-tuple-element.1363), channel_id=1, source_target_pairs={{0,1},{1,2},{2,3},{3,4},{4,5},{5,6},{6,7},{7,8},{8,9},{9,10},{10,1... | collective-permute-start | bytes 1572872 | tf_op jit(solution)/shard_map/while/body/eval_jaxpr/ppermute | solution.py:88
  822.3 27.2 %collective-permute-start.9 = (f32[16,64,128]{2,1,0:T(8,128)S(1)}, f32[16,64,128]{2,1,0:T(8,128)}, u32[]{:S(2)}, u32[]{:S(2)}) collective-permute-start(f32[16,64,128]{2,1,0:T(8,128)S(1)} %get-tuple-element.1363), channel_id=1, source_target_pairs={{0,1},{1,2},{2,3},{3,4},{4,5},{5,6},{6,7},{7,8},{8,9},{9,10},{10,1... | collective-permute-start | bytes 1572872 | tf_op jit(solution)/shard_map/while/body/eval_jaxpr/ppermute | solution.py:88
  857.4 24.1 %collective-permute-start.8 = (f32[16,64,128]{2,1,0:T(8,128)}, f32[16,64,128]{2,1,0:T(8,128)}, u32[]{:S(2)}, u32[]{:S(2)}) collective-permute-start(f32[16,64,128]{2,1,0:T(8,128)} %get-tuple-element.1362), channel_id=1, source_target_pairs={{0,1},{1,2},{2,3},{3,4},{4,5},{5,6},{6,7},{7,8},{8,9},{9,10},{10,1... | collective-permute-start | bytes 1572872 | tf_op jit(solution)/shard_map/while/body/eval_jaxpr/ppermute | solution.py:87
  858.7 27.2 %collective-permute-start.9 = (f32[16,64,128]{2,1,0:T(8,128)S(1)}, f32[16,64,128]{2,1,0:T(8,128)}, u32[]{:S(2)}, u32[]{:S(2)}) collective-permute-start(f32[16,64,128]{2,1,0:T(8,128)S(1)} %get-tuple-element.1363), channel_id=1, source_target_pairs={{0,1},{1,2},{2,3},{3,4},{4,5},{5,6},{6,7},{7,8},{8,9},{9,10},{10,1... | collective-permute-start | bytes 1572872 | tf_op jit(solution)/shard_map/while/body/eval_jaxpr/ppermute | solution.py:88
  893.9 24.1 %collective-permute-start.8 = (f32[16,64,128]{2,1,0:T(8,128)}, f32[16,64,128]{2,1,0:T(8,128)}, u32[]{:S(2)}, u32[]{:S(2)}) collective-permute-start(f32[16,64,128]{2,1,0:T(8,128)} %get-tuple-element.1362), channel_id=1, source_target_pairs={{0,1},{1,2},{2,3},{3,4},{4,5},{5,6},{6,7},{7,8},{8,9},{9,10},{10,1... | collective-permute-start | bytes 1572872 | tf_op jit(solution)/shard_map/while/body/eval_jaxpr/ppermute | solution.py:87
  895.2 27.2 %collective-permute-start.9 = (f32[16,64,128]{2,1,0:T(8,128)S(1)}, f32[16,64,128]{2,1,0:T(8,128)}, u32[]{:S(2)}, u32[]{:S(2)}) collective-permute-start(f32[16,64,128]{2,1,0:T(8,128)S(1)} %get-tuple-element.1363), channel_id=1, source_target_pairs={{0,1},{1,2},{2,3},{3,4},{4,5},{5,6},{6,7},{7,8},{8,9},{9,10},{10,1... | collective-permute-start | bytes 1572872 | tf_op jit(solution)/shard_map/while/body/eval_jaxpr/ppermute | solution.py:88
  930.4 24.1 %collective-permute-start.8 = (f32[16,64,128]{2,1,0:T(8,128)}, f32[16,64,128]{2,1,0:T(8,128)}, u32[]{:S(2)}, u32[]{:S(2)}) collective-permute-start(f32[16,64,128]{2,1,0:T(8,128)} %get-tuple-element.1362), channel_id=1, source_target_pairs={{0,1},{1,2},{2,3},{3,4},{4,5},{5,6},{6,7},{7,8},{8,9},{9,10},{10,1... | collective-permute-start | bytes 1572872 | tf_op jit(solution)/shard_map/while/body/eval_jaxpr/ppermute | solution.py:87
  931.7 27.2 %collective-permute-start.9 = (f32[16,64,128]{2,1,0:T(8,128)S(1)}, f32[16,64,128]{2,1,0:T(8,128)}, u32[]{:S(2)}, u32[]{:S(2)}) collective-permute-start(f32[16,64,128]{2,1,0:T(8,128)S(1)} %get-tuple-element.1363), channel_id=1, source_target_pairs={{0,1},{1,2},{2,3},{3,4},{4,5},{5,6},{6,7},{7,8},{8,9},{9,10},{10,1... | collective-permute-start | bytes 1572872 | tf_op jit(solution)/shard_map/while/body/eval_jaxpr/ppermute | solution.py:88
  966.9 24.1 %collective-permute-start.8 = (f32[16,64,128]{2,1,0:T(8,128)}, f32[16,64,128]{2,1,0:T(8,128)}, u32[]{:S(2)}, u32[]{:S(2)}) collective-permute-start(f32[16,64,128]{2,1,0:T(8,128)} %get-tuple-element.1362), channel_id=1, source_target_pairs={{0,1},{1,2},{2,3},{3,4},{4,5},{5,6},{6,7},{7,8},{8,9},{9,10},{10,1... | collective-permute-start | bytes 1572872 | tf_op jit(solution)/shard_map/while/body/eval_jaxpr/ppermute | solution.py:87
  968.2 27.2 %collective-permute-start.9 = (f32[16,64,128]{2,1,0:T(8,128)S(1)}, f32[16,64,128]{2,1,0:T(8,128)}, u32[]{:S(2)}, u32[]{:S(2)}) collective-permute-start(f32[16,64,128]{2,1,0:T(8,128)S(1)} %get-tuple-element.1363), channel_id=1, source_target_pairs={{0,1},{1,2},{2,3},{3,4},{4,5},{5,6},{6,7},{7,8},{8,9},{9,10},{10,1... | collective-permute-start | bytes 1572872 | tf_op jit(solution)/shard_map/while/body/eval_jaxpr/ppermute | solution.py:88
  1003.4 24.1 %collective-permute-start.8 = (f32[16,64,128]{2,1,0:T(8,128)}, f32[16,64,128]{2,1,0:T(8,128)}, u32[]{:S(2)}, u32[]{:S(2)}) collective-permute-start(f32[16,64,128]{2,1,0:T(8,128)} %get-tuple-element.1362), channel_id=1, source_target_pairs={{0,1},{1,2},{2,3},{3,4},{4,5},{5,6},{6,7},{7,8},{8,9},{9,10},{10,1... | collective-permute-start | bytes 1572872 | tf_op jit(solution)/shard_map/while/body/eval_jaxpr/ppermute | solution.py:87
  1004.7 27.2 %collective-permute-start.9 = (f32[16,64,128]{2,1,0:T(8,128)S(1)}, f32[16,64,128]{2,1,0:T(8,128)}, u32[]{:S(2)}, u32[]{:S(2)}) collective-permute-start(f32[16,64,128]{2,1,0:T(8,128)S(1)} %get-tuple-element.1363), channel_id=1, source_target_pairs={{0,1},{1,2},{2,3},{3,4},{4,5},{5,6},{6,7},{7,8},{8,9},{9,10},{10,1... | collective-permute-start | bytes 1572872 | tf_op jit(solution)/shard_map/while/body/eval_jaxpr/ppermute | solution.py:88
  1039.9 24.1 %collective-permute-start.8 = (f32[16,64,128]{2,1,0:T(8,128)}, f32[16,64,128]{2,1,0:T(8,128)}, u32[]{:S(2)}, u32[]{:S(2)}) collective-permute-start(f32[16,64,128]{2,1,0:T(8,128)} %get-tuple-element.1362), channel_id=1, source_target_pairs={{0,1},{1,2},{2,3},{3,4},{4,5},{5,6},{6,7},{7,8},{8,9},{9,10},{10,1... | collective-permute-start | bytes 1572872 | tf_op jit(solution)/shard_map/while/body/eval_jaxpr/ppermute | solution.py:87
  1041.2 27.2 %collective-permute-start.9 = (f32[16,64,128]{2,1,0:T(8,128)S(1)}, f32[16,64,128]{2,1,0:T(8,128)}, u32[]{:S(2)}, u32[]{:S(2)}) collective-permute-start(f32[16,64,128]{2,1,0:T(8,128)S(1)} %get-tuple-element.1363), channel_id=1, source_target_pairs={{0,1},{1,2},{2,3},{3,4},{4,5},{5,6},{6,7},{7,8},{8,9},{9,10},{10,1... | collective-permute-start | bytes 1572872 | tf_op jit(solution)/shard_map/while/body/eval_jaxpr/ppermute | solution.py:88
  1076.4 24.1 %collective-permute-start.8 = (f32[16,64,128]{2,1,0:T(8,128)}, f32[16,64,128]{2,1,0:T(8,128)}, u32[]{:S(2)}, u32[]{:S(2)}) collective-permute-start(f32[16,64,128]{2,1,0:T(8,128)} %get-tuple-element.1362), channel_id=1, source_target_pairs={{0,1},{1,2},{2,3},{3,4},{4,5},{5,6},{6,7},{7,8},{8,9},{9,10},{10,1... | collective-permute-start | bytes 1572872 | tf_op jit(solution)/shard_map/while/body/eval_jaxpr/ppermute | solution.py:87
  1077.7 27.2 %collective-permute-start.9 = (f32[16,64,128]{2,1,0:T(8,128)S(1)}, f32[16,64,128]{2,1,0:T(8,128)}, u32[]{:S(2)}, u32[]{:S(2)}) collective-permute-start(f32[16,64,128]{2,1,0:T(8,128)S(1)} %get-tuple-element.1363), channel_id=1, source_target_pairs={{0,1},{1,2},{2,3},{3,4},{4,5},{5,6},{6,7},{7,8},{8,9},{9,10},{10,1... | collective-permute-start | bytes 1572872 | tf_op jit(solution)/shard_map/while/body/eval_jaxpr/ppermute | solution.py:88
  1112.9 24.1 %collective-permute-start.8 = (f32[16,64,128]{2,1,0:T(8,128)}, f32[16,64,128]{2,1,0:T(8,128)}, u32[]{:S(2)}, u32[]{:S(2)}) collective-permute-start(f32[16,64,128]{2,1,0:T(8,128)} %get-tuple-element.1362), channel_id=1, source_target_pairs={{0,1},{1,2},{2,3},{3,4},{4,5},{5,6},{6,7},{7,8},{8,9},{9,10},{10,1... | collective-permute-start | bytes 1572872 | tf_op jit(solution)/shard_map/while/body/eval_jaxpr/ppermute | solution.py:87
  1114.2 27.2 %collective-permute-start.9 = (f32[16,64,128]{2,1,0:T(8,128)S(1)}, f32[16,64,128]{2,1,0:T(8,128)}, u32[]{:S(2)}, u32[]{:S(2)}) collective-permute-start(f32[16,64,128]{2,1,0:T(8,128)S(1)} %get-tuple-element.1363), channel_id=1, source_target_pairs={{0,1},{1,2},{2,3},{3,4},{4,5},{5,6},{6,7},{7,8},{8,9},{9,10},{10,1... | collective-permute-start | bytes 1572872 | tf_op jit(solution)/shard_map/while/body/eval_jaxpr/ppermute | solution.py:88
  1150.7 27.2 %collective-permute-start.9 = (f32[16,64,128]{2,1,0:T(8,128)S(1)}, f32[16,64,128]{2,1,0:T(8,128)}, u32[]{:S(2)}, u32[]{:S(2)}) collective-permute-start(f32[16,64,128]{2,1,0:T(8,128)S(1)} %get-tuple-element.1363), channel_id=1, source_target_pairs={{0,1},{1,2},{2,3},{3,4},{4,5},{5,6},{6,7},{7,8},{8,9},{9,10},{10,1... | collective-permute-start | bytes 1572872 | tf_op jit(solution)/shard_map/while/body/eval_jaxpr/ppermute | solution.py:88
  (209 other events, 1745.1 us)
where the time goes:
time: 1200 us; the launch traced here: 1190 us
  matrix products  636 us (53%)
  starting transfers between devices  248 us (21%)
  waiting for transfers between devices  145 us (12%)
  other arithmetic  132 us (11%)
  local copies, waits for them, and re-layouts  27.3 us (2%)
    dot_general x31, matrix products, masked_scores(): jnp.einsum('crie,cle->cril', query, key_cur, preferred_element_type=jnp.f...  215 us
    dot_general x16, matrix products, out_update(): jnp.einsum('cril,cle->crie', prob_bf16, val_cur, preferred_element_type=j...  154 us
    dot_general x16, matrix products, grad_update(): jnp.einsum('crie,cle->cril', grad_out, val_cur, preferred_element_type=jn...  137 us
    reduce_sum x16, other arithmetic, stats_update(): jnp.sum(exp_scores, axis=-1)  94.3 us
    ppermute x15, waiting for transfers between devices, stats_body(): doc_cur = lax.ppermute(doc_cur, 'cp', to_next)  84.2 us
    dot_general x16, matrix products, grad_update(): jnp.einsum('cril,crie->cle', grad_score, query, preferred_element_type=jn...  58 us
    dot_general x16, matrix products, grad_update(): jnp.einsum('cril,crie->cle', prob_bf16, grad_out, preferred_element_type=...  45 us
    ppermute x15, waiting for transfers between devices, out_body(): doc_cur = lax.ppermute(doc_cur, 'cp', to_next)  42.2 us
  transfers between devices with their start and end apart: 152, of which 90 were waited for; matrix products, arithmetic and copies ran while one was open for 31% of the time, Pallas kernels for 0%

commit v1 on v0

v1 whole, which is shorter than its diff:
```python
import functools

import jax
import jax.numpy as jnp
from jax import lax
from jax.experimental import pallas as pl
from jax.experimental.pallas import tpu as pltpu
from jax.sharding import PartitionSpec as P

LOG2E = 1.4426950408889634
MASKED = -3e38
UNMASKED = 3e38
KEY_BLOCK = 256
ROW_BLOCK = 256
NT = (((1,), (1,)), ((), ()))


def attention_kernel(n_chunk, meta, q_ref, g_ref, kv_ref, doc_row_ref, doc_col_ref, o_ref, dq_ref, dkv_ref,
                     s_scr, stat_scr, inv_scr, acc_scr, p_scr, ds_scr, qt_scr, gt_scr):
    b = pl.program_id(0)
    n_dev, _, piece, wide = kv_ref.shape
    head_dim = wide // 2
    n_heads = q_ref.shape[2]
    rows = piece * n_heads
    per_block = KEY_BLOCK // piece
    n_blocks = n_dev * piece // KEY_BLOCK
    n_rows = rows // ROW_BLOCK
    toks = ROW_BLOCK // n_heads
    scale = head_dim ** -0.5
    lo = meta[b]
    rank = meta[n_chunk]
    hi = (rank * piece + piece + KEY_BLOCK - 1) // KEY_BLOCK
    f32 = jnp.float32
    bf16 = jnp.bfloat16

    def load_rows(ref, c):
        return ref[0, c * toks:(c + 1) * toks].reshape(ROW_BLOCK, head_dim)

    def keys_at(kb):
        blk = kv_ref[pl.ds(kb * per_block, per_block), 0, :, :head_dim]
        return blk.reshape(KEY_BLOCK, head_dim)

    def vals_at(kb):
        blk = kv_ref[pl.ds(kb * per_block, per_block), 0, :, head_dim:]
        return blk.reshape(KEY_BLOCK, head_dim)

    for c in range(n_rows):
        sl = slice(c * ROW_BLOCK, (c + 1) * ROW_BLOCK)
        qt_scr[:, sl] = load_rows(q_ref, c).T
        gt_scr[:, sl] = load_rows(g_ref, c).T

    stat_scr[...] = jnp.full(stat_scr.shape, MASKED, f32)

    def score_step(kb, carry):
        key = keys_at(kb)
        col = kb * KEY_BLOCK + lax.broadcasted_iota(jnp.int32, (piece, KEY_BLOCK), 1)
        row = rank * piece + lax.broadcasted_iota(jnp.int32, (piece, KEY_BLOCK), 0)
        doc_k = doc_row_ref[0, :, pl.ds(kb * KEY_BLOCK, KEY_BLOCK)]
        doc_q = doc_col_ref[0]
        doc_q = jnp.concatenate([doc_q] * (KEY_BLOCK // doc_q.shape[1]), axis=1)
        visible = (col <= row) & (doc_q == doc_k)
        limit = jnp.where(visible, UNMASKED, MASKED)
        for c in range(n_rows):
            sl = slice(c * ROW_BLOCK, (c + 1) * ROW_BLOCK)
            raw = lax.dot_general(load_rows(q_ref, c), key, NT, preferred_element_type=f32)
            lim = limit[c * toks:(c + 1) * toks]
            raw = jnp.minimum(raw.reshape(toks, n_heads, KEY_BLOCK), lim[:, None, :]).reshape(ROW_BLOCK, KEY_BLOCK)
            s_scr[kb, sl, :] = raw
            top = stat_scr[sl]
            for p in range(KEY_BLOCK // 128):
                top = jnp.maximum(top, raw[:, p * 128:(p + 1) * 128])
            stat_scr[sl] = top
        return carry

    lax.fori_loop(lo, hi, score_step, 0)
    for c in range(n_rows):
        sl = slice(c * ROW_BLOCK, (c + 1) * ROW_BLOCK)
        stat_scr[sl] = jnp.broadcast_to(jnp.max(stat_scr[sl], axis=1, keepdims=True), (ROW_BLOCK, 128))
    inv_scr[...] = jnp.zeros(inv_scr.shape, f32)

    def exp_step(kb, carry):
        for c in range(n_rows):
            sl = slice(c * ROW_BLOCK, (c + 1) * ROW_BLOCK)
            top = stat_scr[sl]
            total = inv_scr[sl]
            for p in range(KEY_BLOCK // 128):
                lanes = slice(p * 128, (p + 1) * 128)
                e = jnp.exp2((s_scr[kb, sl, lanes] - top) * (scale * LOG2E))
                s_scr[kb, sl, lanes] = e
                total = total + e
            inv_scr[sl] = total
        return carry

    lax.fori_loop(lo, hi, exp_step, 0)
    for c in range(n_rows):
        sl = slice(c * ROW_BLOCK, (c + 1) * ROW_BLOCK)
        inv_scr[sl] = jnp.broadcast_to(1.0 / jnp.sum(inv_scr[sl], axis=1, keepdims=True), (ROW_BLOCK, 128))
    acc_scr[...] = jnp.zeros(acc_scr.shape, f32)

    def out_step(kb, carry):
        val = vals_at(kb)
        for c in range(n_rows):
            sl = slice(c * ROW_BLOCK, (c + 1) * ROW_BLOCK)
            inv = inv_scr[sl]
            parts = []
            for p in range(KEY_BLOCK // 128):
                lanes = slice(p * 128, (p + 1) * 128)
                prob = s_scr[kb, sl, lanes] * inv
                s_scr[kb, sl, lanes] = prob
                parts.append(prob.astype(bf16))
            acc_scr[sl] += jnp.dot(jnp.concatenate(parts, axis=1), val, preferred_element_type=f32)
        return carry

    lax.fori_loop(lo, hi, out_step, 0)
    for c in range(n_rows):
        sl = slice(c * ROW_BLOCK, (c + 1) * ROW_BLOCK)
        out = acc_scr[sl].astype(bf16)
        o_ref[0, c * toks:(c + 1) * toks] = out.reshape(toks, n_heads, head_dim)
        delta = jnp.sum(load_rows(g_ref, c).astype(f32) * out.astype(f32), axis=1, keepdims=True)
        stat_scr[sl] = jnp.broadcast_to(delta, (ROW_BLOCK, 128))
    acc_scr[...] = jnp.zeros(acc_scr.shape, f32)

    def grad_step(kb, carry):
        key = keys_at(kb)
        val = vals_at(kb)
        for c in range(n_rows):
            sl = slice(c * ROW_BLOCK, (c + 1) * ROW_BLOCK)
            gp = lax.dot_general(load_rows(g_ref, c), val, NT, preferred_element_type=f32)
            delta = stat_scr[sl]
            parts = []
            for p in range(KEY_BLOCK // 128):
                lanes = slice(p * 128, (p + 1) * 128)
                prob = s_scr[kb, sl, lanes]
                p_scr[sl, lanes] = prob.astype(bf16)
                parts.append((prob * (gp[:, lanes] - delta)).astype(bf16))
            ds = jnp.concatenate(parts, axis=1)
            ds_scr[sl, :] = ds
            acc_scr[sl] += jnp.dot(ds, key, preferred_element_type=f32)
        dk_t = jnp.dot(qt_scr[...], ds_scr[...], preferred_element_type=f32)
        dv_t = jnp.dot(gt_scr[...], p_scr[...], preferred_element_type=f32)
        dkv_ref[pl.ds(kb * per_block, per_block), 0, :, :head_dim] = dk_t.T.reshape(per_block, piece, head_dim)
        dkv_ref[pl.ds(kb * per_block, per_block), 0, :, head_dim:] = dv_t.T.reshape(per_block, piece, head_dim)
        return carry

    lax.fori_loop(lo, hi, grad_step, 0)
    for c in range(n_rows):
        sl = slice(c * ROW_BLOCK, (c + 1) * ROW_BLOCK)
        dq_ref[0, c * toks:(c + 1) * toks] = (acc_scr[sl] * scale).astype(bf16).reshape(toks, n_heads, head_dim)

    def zero_step(kb, carry):
        dkv_ref[pl.ds(kb * per_block, per_block)] = jnp.zeros((per_block, 1, piece, wide), f32)
        return carry

    lax.fori_loop(0, lo, zero_step, 0)
    lax.fori_loop(hi, n_blocks, zero_step, 0)


def attention(query, grad_out, kv_all, doc_all, doc_loc, rank):
    n_dev, n_chunk, piece, wide = kv_all.shape
    n_heads, head_dim = query.shape[2:]
    rows = piece * n_heads
    seq = n_dev * piece
    first = jnp.sum((doc_all < doc_loc[:, :1]).astype(jnp.int32), axis=1)
    meta = jnp.concatenate([first // KEY_BLOCK, rank[None].astype(jnp.int32)])
    doc_row = doc_all[:, None, :]
    doc_col = jnp.broadcast_to(doc_loc[:, :, None], (n_chunk, piece, 128))
    tok_spec = pl.BlockSpec((1, piece, n_heads, head_dim), lambda b, m: (b, 0, 0, 0))
    kv_spec = pl.BlockSpec((n_dev, 1, piece, wide), lambda b, m: (0, b, 0, 0))
    f32 = jnp.float32
    bf16 = jnp.bfloat16
    return pl.pallas_call(
        functools.partial(attention_kernel, n_chunk),
        grid_spec=pltpu.PrefetchScalarGridSpec(
            num_scalar_prefetch=1,
            grid=(n_chunk,),
            in_specs=[tok_spec, tok_spec, kv_spec,
                      pl.BlockSpec((1, 1, seq), lambda b, m: (b, 0, 0)),
                      pl.BlockSpec((1, piece, 128), lambda b, m: (b, 0, 0))],
            out_specs=[tok_spec, tok_spec, kv_spec],
            scratch_shapes=[
                pltpu.VMEM((seq // KEY_BLOCK, rows, KEY_BLOCK), f32),
                pltpu.VMEM((rows, 128), f32),
                pltpu.VMEM((rows, 128), f32),
                pltpu.VMEM((rows, head_dim), f32),
                pltpu.VMEM((rows, KEY_BLOCK), bf16),
                pltpu.VMEM((rows, KEY_BLOCK), bf16),
                pltpu.VMEM((head_dim, rows), bf16),
                pltpu.VMEM((head_dim, rows), bf16),
            ]),
        out_shape=[jax.ShapeDtypeStruct(query.shape, bf16),
                   jax.ShapeDtypeStruct(query.shape, bf16),
                   jax.ShapeDtypeStruct((n_dev, n_chunk, piece, wide), f32)],
        cost_estimate=pl.CostEstimate(
            flops=6 * n_chunk * rows * seq * head_dim,
            bytes_accessed=4 * query.size * 2 + kv_all.size * 6,
            transcendentals=n_chunk * rows * seq // 2),
    )(meta, query, grad_out, kv_all, doc_row, doc_col)


def solution(mesh):
    seq_spec = P('dp', 'cp', None, None)
    id_spec = P('dp', 'cp')

    def per_device(query, keys, values, grad_out, doc_id):
        head_dim = query.shape[3]
        rank = lax.axis_index('cp')
        kv_loc = jnp.concatenate([keys[:, :, 0, :], values[:, :, 0, :]], axis=-1)
        kv_all = lax.all_gather(kv_loc, 'cp')
        doc_all = lax.all_gather(doc_id, 'cp', axis=1, tiled=True)
        out, grad_query, dkv = attention(query, grad_out, kv_all, doc_all, doc_id, rank)
        total = lax.psum_scatter(dkv, 'cp', scatter_dimension=0)
        grad_keys = (total[:, :, :head_dim] * head_dim ** -0.5).astype(jnp.bfloat16)[:, :, None, :]
        grad_values = total[:, :, head_dim:].astype(jnp.bfloat16)[:, :, None, :]
        return out, grad_query, grad_keys, grad_values

    return jax.shard_map(per_device, mesh=mesh, in_specs=(seq_spec, seq_spec, seq_spec, seq_spec, id_spec), out_specs=(seq_spec, seq_spec, seq_spec, seq_spec), check_vma=False)
```

time: 1200 us -> 267 us (0.22)
  matrix products: 636 us -> 0 us
  starting transfers between devices: 248 us -> 0.13 us
  other arithmetic: 132 us -> 4.56 us
  Pallas kernels: 0 us -> 44.8 us
  waiting for transfers between devices: 145 us -> 173 us
  blocking collectives: 0 us -> 23.4 us
  local copies, waits for them, and re-layouts: 27.3 us -> 5.16 us
  between operations: 0.78 us -> 14.1 us
    dot_general x111 -> x0, matrix products: 636 us -> none  [the longest x31 215 us: masked_scores(): jnp.einsum('crie,cle->cril', query, key_cur, preferred_element_type=jnp.f...]
    ppermute x152 -> x0, starting transfers between devices: 248 us -> none  [the longest x15 37.6 us: grad_body(): doc_cur = lax.ppermute(doc_cur, 'cp', to_next)]
    ppermute x152 -> x0, waiting for transfers between devices: 145 us -> none  [the longest x15 84.2 us: stats_body(): doc_cur = lax.ppermute(doc_cur, 'cp', to_next)]
    reduce_scatter x0 -> x1, waiting for transfers between devices: none -> 140 us  [per_device(): total = lax.psum_scatter(dkv, 'cp', scatter_dimension=0)]
    reduce_sum x16 -> x1, other arithmetic: 94.3 us -> 0.19 us  [attention(): first = jnp.sum((doc_all < doc_loc[:, :1]).astype(jnp.int32), axis=1)]
    pallas_call x0 -> x1, Pallas kernels: none -> 44.8 us  [attention(): pl.pallas_call(functools.partial(attention_kernel, n_chunk), grid_spec=pl...]
    all_gather x0 -> x1, waiting for transfers between devices: none -> 32.8 us  [per_device(): kv_all = lax.all_gather(kv_loc, 'cp')]
    all_gather x0 -> x1, blocking collectives: none -> 23.4 us  [per_device(): doc_all = lax.all_gather(doc_id, 'cp', axis=1, tiled=True)]
  transfers between devices with their start and end apart: 152 -> 2, of which waited for: 90 -> 2; matrix products, arithmetic and copies ran while one was open for 31% -> 1% of each run, Pallas kernels for 0% -> 0%
where the time goes in v1:
time: 267 us; the launch traced here: 265 us
  waiting for transfers between devices  173 us (65%)
  Pallas kernels  44.8 us (17%)
  blocking collectives  23.4 us (9%)
  between operations  14.1 us (5%)
  local copies, waits for them, and re-layouts  5.16 us (2%)
  other arithmetic  4.56 us (2%)
    reduce_scatter x1, waiting for transfers between devices, per_device(): total = lax.psum_scatter(dkv, 'cp', scatter_dimension=0)  140 us
    pallas_call x1, Pallas kernels, attention(): pl.pallas_call(functools.partial(attention_kernel, n_chunk), grid_spec=pl...  44.8 us
    all_gather x1, waiting for transfers between devices, per_device(): kv_all = lax.all_gather(kv_loc, 'cp')  32.8 us
    all_gather x1, blocking collectives, per_device(): doc_all = lax.all_gather(doc_id, 'cp', axis=1, tiled=True)  23.4 us
  transfers between devices with their start and end apart: 2, of which 2 were waited for; matrix products, arithmetic and copies ran while one was open for 1% of the time, Pallas kernels for 0%

profile of v1, /device:TPU:21, one launch (start us, length us, event | category | flops | bytes accessed | tf_op | source)
XLA Modules:
  0.0 265.1 jit_solution(1259485781620958919)
XLA Ops:
  7.2 0.1 all-gather.4.cloned.1.call-start
  7.2 1.9 pad_maximum_fusion
  9.1 0.1 all-gather.4.cloned.1.call-update
  9.2 0.1 reduce-scatter.2.cloned.1.call-start
  9.3 23.4 %all-gather.1 = s32[16,64,16]{1,2,0:T(8,128)S(1)} all-gather(s32[1,64,16]{1,2,0:T(8,128)} %bitcast.25), channel_id=1, replica_groups=mesh['dp'=4,'cp'=16] {'cp'}, dimensions={0}, use_global_device_ids=true | all-gather | bytes 69632 | tf_op jit(solution)/shard_map/all_gather | solution.py:209
  32.7 0.1 reshape.11
  32.8 0.7 broadcast_in_dim.19.doc_row_ref
  33.5 0.8 slice_reduce_fusion
  34.3 0.2 convert_reduce_fusion
  34.5 0.6 pad_add_fusion.meta
  35.2 32.8 %all-gather.4.cloned.1.call-done = bf16[256,64,256]{2,1,0:T(8,128)(2,1)} async-done(((bf16[16,64,256]{2,1,0:T(8,128)(2,1)}), bf16[256,64,256]{2,1,0:T(8,128)(2,1)}) %all-gather.4.cloned.1.call-update) | async-done | bytes 8388624 | tf_op jit(solution)/shard_map/all_gather | solution.py:208
  68.0 1.7 broadcast_in_dim.20.doc_col_ref
  69.8 44.8 %shard_map.84 = (bf16[16,64,16,128]{3,2,1,0:T(8,128)(2,1)}, bf16[16,64,16,128]{3,2,1,0:T(8,128)(2,1)}, f32[16,16,64,256]{3,2,1,0:T(8,128)}) custom-call(s32[17]{0:T(128)} %pad_add_fusion.meta, bf16[16,64,16,128]{3,2,1,0:T(8,128)(2,1)} %q_ref.1, bf16[16,64,16,128]{3,2,1,0:T(8,128)(2,1)} %g_ref.1, bf16[16,16,64,256]{3,2,1,0:T(8,128)(2,1)} %bitcast.26, ...), custom_call_target="tpu_custom_call" | custom-call | flops 12884901888 | bytes 41943040 | tf_op jit(solution)/shard_map/pallas_call | solution.py:171
  114.5 0.1 reduce-scatter.2.cloned.1.call-update
  114.6 140.1 %reduce-scatter.2.cloned.1.call-done = f32[1,16,64,256]{3,2,1,0:T(8,128)} async-done(((f32[16,16,64,256]{3,2,1,0:T(8,128)}), f32[1,16,64,256]{3,2,1,0:T(8,128)}) %reduce-scatter.2.cloned.1.call-update) | async-done | bytes 1048592 | tf_op jit(solution)/shard_map/reduce_scatter | solution.py:211
  254.7 1.8 fusion.2
  256.5 1.8 fusion.1
  (2 shorter events, 0.1 us)
Async XLA Ops:
  7.2 60.8 %all-gather.4.cloned.1.call-start = ((), (), s32[]{:S(2)}) async-start(), calls=%async_computation.2 | async-start | bytes 8912896 | tf_op jit(solution)/shard_map/all_gather | solution.py:208
  9.2 245.5 %reduce-scatter.2.cloned.1.call-start = ((), (), s32[]{:S(2)}) async-start(), calls=%async_computation.1 | async-start | bytes 17825792 | tf_op jit(solution)/shard_map/reduce_scatter | solution.py:211
Sparse Core Ops, SparseCore 0:
  10.2 57.7 all-gather.3
  114.7 139.9 reduce-scatter.1

commit v2 on v1

v2 whole, which is shorter than its diff:
```python
import functools

import jax
import jax.numpy as jnp
from jax import lax
from jax.experimental import pallas as pl
from jax.experimental.pallas import tpu as pltpu
from jax.sharding import PartitionSpec as P

LOG2E = 1.4426950408889634
MASKED = -3e38
UNMASKED = 3e38
KEY_BLOCK = 256
MESH = pl.DeviceIdType.MESH


def fused_kernel(q_ref, g_ref, kv_ref, doc_ref, doc_col_ref, o_ref, dq_ref, dkv_ref,
                 kv_all, doc_all, part, pair_in, down_in, up_in, last_in, swap_out, swap_in,
                 s_scr, stat_scr, inv_scr, acc_scr, p_scr, ds_scr, qt_scr, gt_scr,
                 g_send, g_recv, f_send, f_recv, d_send, d_recv, x_send, x_recv,
                 dn_send, dn_recv, up_send, up_recv, last_recv, sw_send, sw_recv):
    t = pl.program_id(0)
    n_seq, n_dev, piece, wide = kv_all.shape
    head_dim = wide // 2
    n_heads = q_ref.shape[2]
    rows = piece * n_heads
    row_block = min(rows, 512)
    n_rows = rows // row_block
    toks = row_block // n_heads
    per_block = KEY_BLOCK // piece
    scale = head_dim ** -0.5
    base = scale * LOG2E
    n_chip = n_dev // 2
    half = n_chip // 2
    f32 = jnp.float32
    bf16 = jnp.bfloat16
    rank = lax.axis_index('cp')
    chip = rank // 2
    core = rank % 2
    partner = chip * 2 + (1 - core)
    hi = (rank * piece + piece + KEY_BLOCK - 1) // KEY_BLOCK

    def lane_of(other):
        return other * 2 + core

    def rcopy(src, dst, ssem, rsem, dev):
        return pltpu.make_async_remote_copy(src_ref=src, dst_ref=dst, send_sem=ssem, recv_sem=rsem,
                                            device_id={'cp': dev}, device_id_type=MESH)

    def each(lower, upper, body):
        def step(i, carry):
            body(i)
            return carry
        lax.fori_loop(lower, upper, step, 0)

    def own_send(b, dst_chip, slot):
        return rcopy(kv_ref.at[b], kv_all.at[b, rank], g_send.at[b, slot], g_recv.at[b, chip], lane_of(dst_chip))

    def pass_on(b, src_chip, dst_chip):
        piece_ref = kv_all.at[b, lane_of(src_chip)]
        return rcopy(piece_ref, piece_ref, g_send.at[b, src_chip], g_recv.at[b, src_chip], lane_of(dst_chip))

    def gather_arrival(b, src_chip):
        slot = kv_all.at[b, lane_of(src_chip)]
        return rcopy(slot, slot, g_send.at[b, src_chip], g_recv.at[b, src_chip], partner)

    def forward_copy(b, src_chip):
        slot = kv_all.at[b, lane_of(src_chip)]
        return rcopy(slot, slot, f_send.at[b, src_chip], f_recv.at[b, src_chip], partner)

    def own_copy(b):
        return rcopy(kv_ref.at[b], kv_all.at[b, rank], f_send.at[b, chip], f_recv.at[b, chip], partner)

    def forward_arrival(b, src_chip):
        slot = kv_all.at[b, src_chip * 2 + (1 - core)]
        return rcopy(slot, slot, f_send.at[b, src_chip], f_recv.at[b, src_chip], partner)

    def doc_copy(dst):
        return rcopy(doc_ref, doc_all.at[rank], d_send.at[dst], d_recv.at[rank], dst)

    def doc_arrival(src):
        return rcopy(doc_ref, doc_all.at[src], d_send.at[src], d_recv.at[src], partner)

    def pair_copy(b):
        return rcopy(part.at[1 - core], pair_in.at[b], x_send.at[b], x_recv.at[b], partner)

    def block_at(b, owner):
        return pair_in.at[b, pl.ds(owner * 2, 2)]

    def down_copy(b, dist):
        return rcopy(block_at(b, chip - dist), down_in.at[b, dist - 1], dn_send.at[b, dist - 1],
                     dn_recv.at[b, dist - 1], lane_of(chip - 1))

    def down_arrival(b, dist):
        slot = down_in.at[b, dist]
        return rcopy(slot, slot, dn_send.at[b, dist], dn_recv.at[b, dist], partner)

    def up_copy(b, dist):
        return rcopy(block_at(b, chip - dist), up_in.at[b, dist - half], up_send.at[b, dist - half],
                     up_recv.at[b, dist - half], lane_of(chip + 1))

    def up_arrival(b, dist):
        slot = up_in.at[b, dist - half - 1]
        return rcopy(slot, slot, up_send.at[b, dist - half - 1], up_recv.at[b, dist - half - 1], partner)

    def last_copy(b, dist):
        return rcopy(block_at(b, chip - dist), last_in.at[b], up_send.at[b, dist - half], last_recv.at[b],
                     lane_of(chip - dist))

    def last_arrival(b):
        slot = last_in.at[b]
        return rcopy(slot, slot, sw_send, last_recv.at[b], partner)

    def swap_copy():
        return rcopy(swap_out.at[1 - core], swap_in, sw_send, sw_recv, partner)

    far = n_chip - 1
    reach = half
    n_far = n_chip - 1 - reach

    def gather_round(when):
        for hop in range(reach + 1):
            b = when + 2 + reach - hop

            @pl.when((b >= 0) & (b < n_seq))
            def _(b=b, hop=hop):
                if hop == 0:
                    own_copy(b).start()

                    @pl.when(chip < far)
                    def _():
                        own_send(b, chip + 1, chip).start()

                    @pl.when(chip < n_far)
                    def _():
                        own_send(b, far, n_chip).start()
                    return

                @pl.when(chip >= hop)
                def _():
                    src = chip - hop
                    gather_arrival(b, src).wait_recv()
                    forward_copy(b, src).start()
                    if hop < reach:
                        @pl.when(chip < far)
                        def _():
                            pass_on(b, src, chip + 1).start()

                if hop <= n_far:
                    @pl.when(chip == n_chip - hop)
                    def _():
                        for src in range(n_far + 1 - hop):
                            gather_arrival(b, src).wait_recv()
                            forward_copy(b, src).start()
                            if src < n_far - hop:
                                pass_on(b, src, far - hop).start()

    def gather_drain(b):
        own_copy(b).wait_send()

        @pl.when(chip < far)
        def _():
            own_send(b, chip + 1, chip).wait_send()

        @pl.when(chip < n_far)
        def _():
            own_send(b, far, n_chip).wait_send()
        for hop in range(1, reach + 1):
            @pl.when(chip >= hop)
            def _(hop=hop):
                forward_copy(b, chip - hop).wait_send()
                if hop < reach:
                    @pl.when(chip < far)
                    def _():
                        pass_on(b, chip - hop, chip + 1).wait_send()
        for hop in range(1, n_far + 1):
            @pl.when(chip == n_chip - hop)
            def _(hop=hop):
                for src in range(n_far + 1 - hop):
                    forward_copy(b, src).wait_send()
                    if src < n_far - hop:
                        pass_on(b, src, far - hop).wait_send()

    @pl.when(t == 0)
    def _():
        kv_all[...] = jnp.zeros(kv_all.shape, bf16)
        doc_all[...] = jnp.zeros(doc_all.shape, jnp.int32)
        kv_all[:, pl.ds(rank, 1)] = kv_ref[...][:, None]
        doc_all[pl.ds(rank, 1)] = doc_ref[...][None]
        barrier = pltpu.get_barrier_semaphore()
        each(1, n_dev, lambda i: pl.semaphore_signal(barrier, inc=1, device_id={'cp': lax.rem(rank + i, n_dev)},
                                                     device_id_type=MESH))
        pl.semaphore_wait(barrier, n_dev - 1)
        each(rank + 1, n_dev, lambda dst: doc_copy(dst).start())

        each(-reach - 2, -1, gather_round)
        each(0, rank, lambda src: doc_arrival(src).wait_recv())
        gather_round(-1)

    def load_rows(ref, c):
        return ref[0, c * toks:(c + 1) * toks].reshape(row_block, head_dim)

    def keys_at(kb):
        return kv_all[t, pl.ds(kb * per_block, per_block), :, :head_dim].reshape(KEY_BLOCK, head_dim)

    def vals_at(kb):
        return kv_all[t, pl.ds(kb * per_block, per_block), :, head_dim:].reshape(KEY_BLOCK, head_dim)

    def score_block(kb):
        key_t = keys_at(kb).T
        doc_q = doc_col_ref[0]
        limits = []
        for p in range(KEY_BLOCK // 128):
            col = kb * KEY_BLOCK + p * 128 + lax.broadcasted_iota(jnp.int32, (piece, 128), 1)
            row = rank * piece + lax.broadcasted_iota(jnp.int32, (piece, 128), 0)
            src = kb * per_block + 2 * p
            doc_k = doc_all[src, pl.ds(t, 1)] + doc_all[src + 1, pl.ds(t, 1)]
            limits.append(jnp.where((col <= row) & (doc_q == doc_k), UNMASKED, MASKED))
        limit = jnp.concatenate(limits, axis=1)
        for c in range(n_rows):
            sl = slice(c * row_block, (c + 1) * row_block)
            raw = jnp.dot(load_rows(q_ref, c), key_t, preferred_element_type=f32)
            lim = limit[c * toks:(c + 1) * toks]
            raw = jnp.minimum((raw * base).reshape(toks, n_heads, KEY_BLOCK), lim[:, None, :]).reshape(row_block, KEY_BLOCK)
            s_scr[kb, sl, :] = raw
            old = stat_scr[sl]
            top = old
            for p in range(KEY_BLOCK // 128):
                top = jnp.maximum(top, raw[:, p * 128:(p + 1) * 128])
            total = inv_scr[sl] * jnp.exp2(old - top)
            for p in range(KEY_BLOCK // 128):
                total = total + jnp.exp2(raw[:, p * 128:(p + 1) * 128] - top)
            stat_scr[sl] = top
            inv_scr[sl] = total

    def out_block(kb, first):
        val = vals_at(kb)
        for c in range(n_rows):
            sl = slice(c * row_block, (c + 1) * row_block)
            norm = inv_scr[sl]
            parts = []
            for p in range(KEY_BLOCK // 128):
                lanes = slice(p * 128, (p + 1) * 128)
                prob = jnp.exp2(s_scr[kb, sl, lanes] - norm)
                s_scr[kb, sl, lanes] = prob
                parts.append(prob.astype(bf16))
            term = jnp.dot(jnp.concatenate(parts, axis=1), val, preferred_element_type=f32)
            acc_scr[sl] = term if first else acc_scr[sl] + term

    def grad_block(kb, first):
        key = keys_at(kb)
        val_t = vals_at(kb).T
        for c in range(n_rows):
            sl = slice(c * row_block, (c + 1) * row_block)
            gp = jnp.dot(load_rows(g_ref, c), val_t, preferred_element_type=f32)
            delta = stat_scr[sl]
            parts = []
            for p in range(KEY_BLOCK // 128):
                lanes = slice(p * 128, (p + 1) * 128)
                prob = s_scr[kb, sl, lanes]
                p_scr[sl, lanes] = prob.astype(bf16)
                parts.append((prob * (gp[:, lanes] - delta)).astype(bf16))
            ds = jnp.concatenate(parts, axis=1)
            ds_scr[sl, :] = ds
            term = jnp.dot(ds, key, preferred_element_type=f32)
            acc_scr[sl] = term if first else acc_scr[sl] + term
        dk_t = jnp.dot(qt_scr[...], ds_scr[...], preferred_element_type=f32)
        dv_t = jnp.dot(gt_scr[...], p_scr[...], preferred_element_type=f32)
        part[0, pl.ds(kb * per_block, per_block)] = dk_t.T.reshape(per_block, piece, head_dim)
        part[1, pl.ds(kb * per_block, per_block)] = dv_t.T.reshape(per_block, piece, head_dim)

    @pl.when(t < n_seq)
    def _():
        each(0, chip + 1, lambda src: forward_arrival(t, src).wait_recv())
        stat_scr[...] = jnp.full(stat_scr.shape, MASKED, f32)
        inv_scr[...] = jnp.zeros(inv_scr.shape, f32)
        each(0, hi - 1, score_block)
        for c in range(n_rows):
            sl = slice(c * row_block, (c + 1) * row_block)
            qt_scr[:, sl] = load_rows(q_ref, c).T
            gt_scr[:, sl] = load_rows(g_ref, c).T
        score_block(hi - 1)
        for c in range(n_rows):
            sl = slice(c * row_block, (c + 1) * row_block)
            old = stat_scr[sl]
            top = jnp.max(old, axis=1, keepdims=True)
            total = jnp.sum(inv_scr[sl] * jnp.exp2(old - top), axis=1, keepdims=True)
            inv_scr[sl] = jnp.broadcast_to(top + jnp.log2(total), (row_block, 128))
        out_block(hi - 1, True)


    final = half + 1

    def stage():
        for step in range(1, final + 1):
            lag = step
            live = (t >= lag) & (t < n_seq + lag)
            b = t - lag
            if step == 1:
                @pl.when(live)
                def _(b=b):
                    pair_copy(b).wait()

                    def add_own(owner):
                        sl = pl.ds(owner * 2, 2)
                        pair_in[b, sl] += part[core, sl]
                    each(0, chip + 1, add_own)
            for dist in (half + step - 1, half - step):
                if dist < 1 or dist >= n_chip:
                    continue

                @pl.when(live & (chip >= dist))
                def _(b=b, dist=dist):
                    owner = pl.ds((chip - dist) * 2, 2)
                    if dist < half:
                        if dist < half - 1:
                            @pl.when(chip < n_chip - 1)
                            def _():
                                down_arrival(b, dist).wait_recv()
                                pair_in[b, owner] += down_in[b, dist]
                        down_copy(b, dist).start()
                    else:
                        if dist > half:
                            up_arrival(b, dist).wait_recv()
                            pair_in[b, owner] += up_in[b, dist - half - 1]

                        if dist < n_chip - 1:
                            @pl.when(chip < n_chip - 1)
                            def _():
                                up_copy(b, dist).start()

                        @pl.when(chip == n_chip - 1)
                        def _():
                            last_copy(b, dist).start()
            if step == final:
                @pl.when(live)
                def _(b=b):
                    own = pl.ds(chip * 2, 2)

                    @pl.when(chip < n_chip - 1)
                    def _():
                        down_arrival(b, 0).wait_recv()
                        pair_in[b, own] += down_in[b, 0]

                    @pl.when(chip < n_chip - half)
                    def _():
                        last_arrival(b).wait_recv()
                        pair_in[b, own] += last_in[b]

                    factor = jnp.where(core == 0, scale, 1.0).astype(f32)
                    total = (pair_in[b, own] * factor).astype(bf16)
                    swap_out[0, b] = total[0]
                    swap_out[1, b] = total[1]

    stage()

    @pl.when(t < n_seq)
    def _():
        each(0, hi - 1, lambda kb: out_block(kb, False))
        for c in range(n_rows):
            sl = slice(c * row_block, (c + 1) * row_block)
            out = acc_scr[sl].astype(bf16)
            o_ref[0, c * toks:(c + 1) * toks] = out.reshape(toks, n_heads, head_dim)
            delta = jnp.sum(load_rows(g_ref, c).astype(f32) * out.astype(f32), axis=1, keepdims=True)
            stat_scr[sl] = jnp.broadcast_to(delta, (row_block, 128))
        grad_block(hi - 1, True)
        each(0, hi - 1, lambda kb: grad_block(kb, False))
        pair_copy(t).start()
        for c in range(n_rows):
            sl = slice(c * row_block, (c + 1) * row_block)
            dq_ref[0, c * toks:(c + 1) * toks] = (acc_scr[sl] * scale).astype(bf16).reshape(toks, n_heads, head_dim)

    gather_round(t)

    @pl.when(t == n_seq + final - 1)
    def _():
        swap_copy().start()
        dkv_ref[pl.ds(core, 1)] = swap_out[pl.ds(core, 1)]
        swap_copy().wait()
        dkv_ref[pl.ds(1 - core, 1)] = swap_in[...][None]
        each(rank + 1, n_dev, lambda dst: doc_copy(dst).wait_send())

        def drain(b):
            gather_drain(b)
            for dist in range(1, n_chip):
                @pl.when(chip >= dist)
                def _(dist=dist):
                    if dist < half:
                        down_copy(b, dist).wait_send()
                    else:
                        if dist < n_chip - 1:
                            @pl.when(chip < n_chip - 1)
                            def _():
                                up_copy(b, dist).wait_send()

                        @pl.when(chip == n_chip - 1)
                        def _():
                            last_copy(b, dist).wait_send()
        each(0, n_seq, drain)


def fused(query, grad_out, kv_loc, doc_send, doc_col, n_dev):
    n_seq, piece, wide = kv_loc.shape
    n_heads, head_dim = query.shape[2:]
    rows = piece * n_heads
    n_chip = n_dev // 2
    half = n_chip // 2
    seq = n_dev * piece
    f32 = jnp.float32
    bf16 = jnp.bfloat16
    tok_spec = pl.BlockSpec((1, piece, n_heads, head_dim), lambda t: (jnp.minimum(t, n_seq - 1), 0, 0, 0))
    dma = pltpu.SemaphoreType.DMA
    return pl.pallas_call(
        fused_kernel,
        grid=(n_seq + half + 1,),
        in_specs=[tok_spec, tok_spec,
                  pl.BlockSpec(memory_space=pltpu.VMEM),
                  pl.BlockSpec(memory_space=pltpu.VMEM),
                  pl.BlockSpec((1, piece, 128), lambda t: (jnp.minimum(t, n_seq - 1), 0, 0))],
        out_specs=[tok_spec, tok_spec, pl.BlockSpec(memory_space=pltpu.VMEM)],
        out_shape=[jax.ShapeDtypeStruct(query.shape, bf16),
                   jax.ShapeDtypeStruct(query.shape, bf16),
                   jax.ShapeDtypeStruct((2, n_seq, piece, head_dim), bf16)],
        scratch_shapes=[
            pltpu.VMEM((n_seq, n_dev, piece, wide), bf16),
            pltpu.VMEM((n_dev, n_seq, 128), jnp.int32),
            pltpu.VMEM((2, n_dev, piece, head_dim), f32),
            pltpu.VMEM((n_seq, n_dev, piece, head_dim), f32),
            pltpu.VMEM((n_seq, half - 1, 2, piece, head_dim), f32),
            pltpu.VMEM((n_seq, half - 1, 2, piece, head_dim), f32),
            pltpu.VMEM((n_seq, 2, piece, head_dim), f32),
            pltpu.VMEM((2, n_seq, piece, head_dim), bf16),
            pltpu.VMEM((n_seq, piece, head_dim), bf16),
            pltpu.VMEM((seq // KEY_BLOCK, rows, KEY_BLOCK), f32),
            pltpu.VMEM((rows, 128), f32),
            pltpu.VMEM((rows, 128), f32),
            pltpu.VMEM((rows, head_dim), f32),
            pltpu.VMEM((rows, KEY_BLOCK), bf16),
            pltpu.VMEM((rows, KEY_BLOCK), bf16),
            pltpu.VMEM((head_dim, rows), bf16),
            pltpu.VMEM((head_dim, rows), bf16),
            dma((n_seq, n_chip + 1)), dma((n_seq, n_chip)),
            dma((n_seq, n_chip)), dma((n_seq, n_chip)),
            dma((n_dev,)), dma((n_dev,)),
            dma((n_seq,)), dma((n_seq,)),
            dma((n_seq, half - 1)), dma((n_seq, half - 1)),
            dma((n_seq, half)), dma((n_seq, half)),
            dma((n_seq,)), dma, dma,
        ],
        compiler_params=pltpu.CompilerParams(
            collective_id=0, has_side_effects=True, vmem_limit_bytes=42 * 1024 * 1024,
            dimension_semantics=('arbitrary',)),
    )(query, grad_out, kv_loc, doc_send, doc_col)


def solution(mesh):
    n_dev = mesh.shape['cp']
    seq_spec = P('dp', 'cp', None, None)
    id_spec = P('dp', 'cp')

    def per_device(query, keys, values, grad_out, doc_id):
        n_seq, piece = doc_id.shape
        rank = lax.axis_index('cp')
        kv_loc = jnp.concatenate([keys[:, :, 0, :], values[:, :, 0, :]], axis=-1)
        blank = jnp.zeros_like(doc_id)
        doc_send = jnp.where(rank % 2 == 0, jnp.concatenate([doc_id, blank], axis=1), jnp.concatenate([blank, doc_id], axis=1))
        doc_col = jnp.broadcast_to(doc_id[:, :, None], (n_seq, piece, 128))
        out, grad_query, dkv = fused(query, grad_out, kv_loc, doc_send, doc_col, n_dev)
        return out, grad_query, dkv[0][:, :, None, :], dkv[1][:, :, None, :]

    return jax.shard_map(per_device, mesh=mesh, in_specs=(seq_spec, seq_spec, seq_spec, seq_spec, id_spec), out_specs=(seq_spec, seq_spec, seq_spec, seq_spec), check_vma=False)
```

time: 267 us -> 186 us (0.70)
  waiting for transfers between devices: 173 us -> 0 us
  Pallas kernels: 44.8 us -> 178 us
  blocking collectives: 23.4 us -> 0 us
  between operations: 14.1 us -> 0.66 us
    reduce_scatter x1 -> x0, waiting for transfers between devices: 140 us -> none  [per_device(): total = lax.psum_scatter(dkv, 'cp', scatter_dimension=0)]
    pallas_call x1, Pallas kernels: 44.8 us -> 178 us  [fused(): pl.pallas_call(fused_kernel, grid=(n_seq + half + 1,), in_specs=[tok_spec...]
    all_gather x1 -> x0, waiting for transfers between devices: 32.8 us -> none  [per_device(): kv_all = lax.all_gather(kv_loc, 'cp')]
    all_gather x1 -> x0, blocking collectives: 23.4 us -> none  [per_device(): doc_all = lax.all_gather(doc_id, 'cp', axis=1, tiled=True)]
    unnamed x2 -> x3, local copies, waits for them, and re-layouts: 1.89 us -> 4.85 us
  transfers between devices with their start and end apart: 2 -> 0, of which waited for: 2 -> 0; matrix products, arithmetic and copies ran while one was open for 1% -> 0% of each run, Pallas kernels for 0% -> 0%
where the time goes in v2:
time: 186 us
  Pallas kernels  178 us (96%)
  local copies, waits for them, and re-layouts  5.74 us (3%)
  other arithmetic  1.95 us (1%)
    pallas_call x1, Pallas kernels, fused(): pl.pallas_call(fused_kernel, grid=(n_seq + half + 1,), in_specs=[tok_spec...  178 us
    unnamed x3, local copies, waits for them, and re-layouts  4.85 us

profile of v2, /device:TPU:21, one launch (start us, length us, event | category | flops | bytes accessed | tf_op | source)
XLA Modules:
  0.0 186.1 jit_solution(16874608241258970263)
XLA Ops:
  0.6 0.8 pad_select_fusion.doc_ref
  1.5 1.1 pad_maximum_fusion.kv_ref
  2.6 0.9 broadcast_in_dim.2.doc_col_ref
  3.5 177.7 %shard_map.84 = (bf16[16,64,16,128]{3,2,1,0:T(8,128)(2,1)S(1)}, bf16[16,64,16,128]{3,2,1,0:T(8,128)(2,1)S(1)}, bf16[2,16,64,128]{3,2,1,0:T(8,128)(2,1)S(1)}) custom-call(bf16[16,64,16,128]{3,2,1,0:T(8,128)(2,1)} %q_ref.1, bf16[16,64,16,128]{3,2,1,0:T(8,128)(2,1)} %g_ref.1, bf16[16,64,256]{2,1,0:T(8,128)(2,1)S(1)} %pad_maximum_fusion.kv_ref, ...), custom_call_target="tpu_custom_call" | custom-call | tf_op jit(solution)/shard_map/pallas_call | solution.py:413
  181.2 0.8 slice_bitcast_fusion
  182.0 2.0 %copy.13 = bf16[16,64,16,128]{3,2,1,0:T(8,128)(2,1)} copy(bf16[16,64,16,128]{3,2,1,0:T(8,128)(2,1)S(1)} %get-tuple-element.20) | data formatting | bytes 8388608
  184.0 2.0 %copy.14 = bf16[16,64,16,128]{3,2,1,0:T(8,128)(2,1)} copy(bf16[16,64,16,128]{3,2,1,0:T(8,128)(2,1)S(1)} %get-tuple-element.21) | data formatting | bytes 8388608
